TPU v7x, 32 devices: a whole 2x2x4 slice. The times are simulated.
32 devices in a mesh: groups: 2 (over y), rows: 16 (over z, x, core).
Axes of the slice: x: 2, y: 2, z: 4, core: 2. Of those that a mesh axis runs over, the one named last changes fastest.
Arguments:
- pair_repr: bfloat16 [256, 128, 128], P('groups', 'rows'), parts along dimension 0, may hold values from -6 to 6
- single_repr: bfloat16 [256, 384], P(('groups', 'rows')), parts along dimension 0, may hold values from -6 to 6
- residue_index: int32 [256], P('groups'), parts along dimension 0, may hold values from 0 to 47
- chain_index: int32 [256], P('groups'), parts along dimension 0, may hold values from 0 to 3
- complex_index: int32 [256], P('groups'), parts along dimension 0, may hold values from 0 to 7, never falling along the last dimension, each value on 1 to 96 neighbouring positions
- pad_mask: int32 [256], P('groups'), parts along dimension 0, may hold values 0 or 1
- w_query: bfloat16 [384, 384], replicated, may hold values from -3 to 3
- w_key: bfloat16 [384, 384], replicated, may hold values from -3.1 to 3.1
- w_value: bfloat16 [384, 384], replicated, may hold values from -0.3125 to 0.3125
- w_gate: bfloat16 [384, 384], replicated, may hold values from -0.3125 to 0.3125
- w_out: bfloat16 [384, 384], replicated, may hold values from -2.5 to 2.5
- w_bias: bfloat16 [128, 16], replicated, may hold values from -0.5 to 0.5
- rel_table: bfloat16 [66, 128], replicated, may hold values from -6 to 6
- w_mix_a: bfloat16 [384, 128], replicated, may hold values from -0.3125 to 0.3125
- w_mix_b: bfloat16 [384, 128], replicated, may hold values from -0.3125 to 0.3125
- w_hidden_a: bfloat16 [128, 512], replicated, may hold values from -0.5 to 0.5
- w_hidden_b: bfloat16 [128, 512], replicated, may hold values from -0.5 to 0.5
- w_hidden_out: bfloat16 [512, 128], replicated, may hold values from -0.25 to 0.25
- w_pae: bfloat16 [128, 64], replicated, may hold values from -30 to 30
- pae_bias: float32 [64], replicated, may hold values from -4 to 4
Outputs:
- refined: bfloat16 [256, 384], P(('groups', 'rows')), parts along dimension 0
- errors: float32 [256, 128], P(('groups', 'rows')), parts along dimension 0
There are 2 independent parts, one for each index of `groups`. A program takes and returns all parts, laid end to end along the dimension named above; an argument that names none is the same for every part. Nothing has to cross between parts.
Inputs may be any that keep to these rules, and one draw needn't show every extreme that they name: `complex_index`: never falls along the tokens; each complex holds 1 to 96 consecutive tokens.
All inputs are finite; a program needn't handle non-finite values.
Results may differ from a plain program's by a relative error of at most 0.023.
Values may be sent and summed in bfloat16 or wider, within the bound.
A program may use at most 128 MiB of HBM per device.

v0:
```python
import math
import jax
import jax.numpy as jnp
from jax import lax
from jax.sharding import PartitionSpec as P

epsilon = 1e-05
masked_score = -1e30


def norm_rows(values):
    center = values - jnp.mean(values, axis=-1, keepdims=True)
    spread = jnp.mean(center * center, axis=-1, keepdims=True)
    return center * lax.rsqrt(spread + epsilon)


def relative(res_query, chain_query, res_key, chain_key, rel_table):
    reach = (rel_table.shape[0] - 2) // 2
    offsets = jnp.clip(res_query[:, None] - res_key[None, :], -reach, reach) + reach
    bucket = jnp.where(chain_query[:, None] == chain_key[None, :], offsets, 2 * reach + 1)
    classes = jnp.arange(rel_table.shape[0], dtype=jnp.int32)
    onehot = (bucket[:, :, None] == classes[None, None, :]).astype(jnp.bfloat16)
    return jnp.einsum("qkr,rc->qkc", onehot, rel_table, preferred_element_type=jnp.float32)


def pair_tail(mixed, w_hidden_a, w_hidden_b, w_hidden_out, w_pae, pae_bias):
    width = mixed.shape[-1]
    flat = mixed.reshape(-1, width)
    normed = norm_rows(flat).astype(jnp.bfloat16)
    gate_part = jnp.dot(normed, w_hidden_a, preferred_element_type=jnp.float32)
    up_part = jnp.dot(normed, w_hidden_b, preferred_element_type=jnp.float32)
    hidden = (jax.nn.silu(gate_part) * up_part).astype(jnp.bfloat16)
    updated = flat + jnp.dot(hidden, w_hidden_out, preferred_element_type=jnp.float32)
    final = norm_rows(updated).astype(jnp.bfloat16)
    logits = jnp.dot(final, w_pae, preferred_element_type=jnp.float32) + pae_bias[None, :]
    probs = jax.nn.softmax(logits, axis=-1)
    bins = w_pae.shape[1]
    centers = (jnp.arange(bins, dtype=jnp.float32) + 0.5) * (32.0 / bins)
    return jnp.sum(probs * centers[None, :], axis=-1).reshape(mixed.shape[:-1])


def on_device(
    pair_repr,
    single_repr,
    residue_index,
    chain_index,
    complex_index,
    pad_mask,
    w_query,
    w_key,
    w_value,
    w_gate,
    w_out,
    w_bias,
    rel_table,
    w_mix_a,
    w_mix_b,
    w_hidden_a,
    w_hidden_b,
    w_hidden_out,
    w_pae,
    pae_bias,
):
    local_rows = single_repr.shape[0]
    head_count = w_bias.shape[1]
    head_size = single_repr.shape[1] // head_count
    first_row = lax.axis_index("rows") * local_rows
    row_ids = first_row + jnp.arange(local_rows, dtype=jnp.int32)
    res_local = lax.dynamic_slice_in_dim(residue_index, first_row, local_rows, 0)
    chain_local = lax.dynamic_slice_in_dim(chain_index, first_row, local_rows, 0)
    complex_local = lax.dynamic_slice_in_dim(complex_index, first_row, local_rows, 0)
    normed = norm_rows(single_repr.astype(jnp.float32)).astype(jnp.bfloat16)
    queries = jnp.dot(normed, w_query, preferred_element_type=jnp.float32).astype(jnp.bfloat16)
    keys_local = jnp.dot(normed, w_key, preferred_element_type=jnp.float32).astype(jnp.bfloat16)
    values_local = jnp.dot(normed, w_value, preferred_element_type=jnp.float32).astype(jnp.bfloat16)
    gating = jax.nn.sigmoid(jnp.dot(normed, w_gate, preferred_element_type=jnp.float32))
    pair_local = lax.all_to_all(pair_repr, "rows", split_axis=0, concat_axis=1, tiled=True)
    pair_in = pair_local.astype(jnp.float32) + relative(
        res_local, chain_local, residue_index, chain_index, rel_table
    )
    pair_bias = jnp.einsum(
        "qkc,ch->hqk",
        norm_rows(pair_in).astype(jnp.bfloat16),
        w_bias,
        preferred_element_type=jnp.float32,
    ).astype(jnp.bfloat16)
    query_heads = queries.reshape(local_rows, head_count, head_size)
    row_max = jnp.full((head_count, local_rows), masked_score, jnp.float32)
    key_part = lax.all_gather(keys_local, "rows", axis=0, tiled=True)
    value_part = lax.all_gather(values_local, "rows", axis=0, tiled=True)
    count = key_part.shape[0]
    key_heads = key_part.reshape(count, head_count, head_size)
    value_heads = value_part.reshape(count, head_count, head_size)
    scores = jnp.einsum(
        "qhd,khd->hqk", query_heads, key_heads, preferred_element_type=jnp.float32
    ) / math.sqrt(head_size)
    scores = scores + pair_bias.astype(jnp.float32)
    key_ids = jnp.arange(count, dtype=jnp.int32)
    allowed = (complex_local[:, None] == complex_index[None, :]) & (
        (pad_mask[None, :] == 1) | (row_ids[:, None] == key_ids[None, :])
    )
    scores = jnp.where(allowed[None], scores, masked_score)
    new_max = jnp.maximum(row_max, jnp.max(scores, axis=-1))
    expo = jnp.exp(scores - new_max[..., None])
    new_sum = jnp.sum(expo, axis=-1)
    added = jnp.einsum(
        "hqk,khd->hqd", expo.astype(jnp.bfloat16), value_heads, preferred_element_type=jnp.float32
    )
    attended = (
        (added / new_sum[..., None]).transpose(1, 0, 2).reshape(local_rows, head_count * head_size)
    )
    refined = (
        single_repr.astype(jnp.float32)
        + jnp.dot(
            (gating * attended).astype(jnp.bfloat16), w_out, preferred_element_type=jnp.float32
        )
    ).astype(jnp.bfloat16)
    renormed = norm_rows(refined.astype(jnp.float32)).astype(jnp.bfloat16)
    factor_a = jnp.dot(renormed, w_mix_a, preferred_element_type=jnp.float32).astype(jnp.bfloat16)
    factor_b = jnp.dot(renormed, w_mix_b, preferred_element_type=jnp.float32).astype(jnp.bfloat16)
    every_b = lax.all_gather(factor_b, "rows", axis=0, tiled=True)
    mixed = (
        pair_in + factor_a.astype(jnp.float32)[:, None, :] * every_b.astype(jnp.float32)[None, :, :]
    )
    errors = pair_tail(mixed, w_hidden_a, w_hidden_b, w_hidden_out, w_pae, pae_bias)
    return (refined, errors)


def solution(mesh):
    placed = (
        P("groups", "rows", None),
        P(("groups", "rows"), None),
        P("groups"),
        P("groups"),
        P("groups"),
        P("groups"),
        P(),
        P(),
        P(),
        P(),
        P(),
        P(),
        P(),
        P(),
        P(),
        P(),
        P(),
        P(),
        P(),
        P(),
    )
    return jax.shard_map(
        on_device,
        mesh=mesh,
        in_specs=placed,
        out_specs=(P(("groups", "rows"), None), P(("groups", "rows"), None)),
        check_vma=False,
    )
```

profile of v0, /device:TPU:0, one launch (start us, length us, event | category | flops | bytes accessed | tf_op | source)
XLA Modules:
  0.0 83.6 jit_solution(17553948313955501287)
XLA Ops:
  0.6 0.0 copy-start
  0.6 0.0 copy-start.7
  0.7 0.0 copy-start.8
  0.7 0.0 copy-start.9
  0.7 0.0 copy-start.3
  0.7 0.0 copy-start.6
  0.7 7.5 %all-to-all-start = ((bf16[128,8,128]{2,1,0:T(8,128)(2,1)}), bf16[128,8,128]{2,1,0:T(8,128)(2,1)S(1)}, u32[]{:S(2)}, u32[]{:S(2)}) async-start(bf16[128,8,128]{2,1,0:T(8,128)(2,1)} %param.20), calls=%async_computation | async-start | bytes 524288 | tf_op jit(solution)/shard_map/all_to_all | solution.py:77
  8.3 0.8 convert_reduce_fusion
  9.1 0.9 %fusion.30 = f32[8]{0:T(128)S(1)} fusion(bf16[8,384]{1,0:T(8,128)(2,1)} %param.21, f32[8]{0:T(128)S(1)} %broadcast_multiply_fusion.4), kind=kLoop, calls=%fused_computation.57 | loop fusion | flops 12280 | bytes 6208 | tf_op jit(solution)/shard_map/reduce_sum | solution.py:13
  10.0 1.2 %convolution_convert_fusion = bf16[8,384]{1,0:T(8,128)(2,1)S(1)} fusion(bf16[384,384]{1,0:T(8,128)(2,1)} %param.28, bf16[8,384]{1,0:T(8,128)(2,1)} %param.21, f32[8]{0:T(128)S(1)} %add_rsqrt_fusion.3, f32[8]{0:T(128)S(1)} %broadcast_multiply_fusion.4), kind=kOutput, calls=%fused_computation.18 | convolution fusion | flops 2374656 | bytes 307264 | tf_op jit(solution)/shard_map/dot_general | solution.py:75
  11.1 22.1 %all_gather.10 = bf16[128,384]{1,0:T(8,128)(2,1)S(1)} all-gather(bf16[8,384]{1,0:T(8,128)(2,1)S(1)} %convolution_convert_fusion), channel_id=1, replica_groups=mesh['groups'=2,'rows'=16] {'rows'}, dimensions={0}, use_global_device_ids=true | all-gather | bytes 104448 | tf_op jit(solution)/shard_map/all_gather | solution.py:90
  33.2 0.1 copy.32
  33.4 0.7 dynamic_slice.11
  34.1 0.7 dynamic_slice.10
  34.8 1.2 %convolution_convert_fusion.1 = bf16[8,384]{1,0:T(8,128)(2,1)S(1)} fusion(bf16[384,384]{1,0:T(8,128)(2,1)} %param.27, bf16[8,384]{1,0:T(8,128)(2,1)} %param.21, f32[8]{0:T(128)S(1)} %add_rsqrt_fusion.3, f32[8]{0:T(128)S(1)} %broadcast_multiply_fusion.4), kind=kOutput, calls=%fused_computation.19 | convolution fusion | flops 2374656 | bytes 307264 | tf_op jit(solution)/shard_map/dot_general | solution.py:74
  36.0 1.2 %convolution_convert_fusion.2 = bf16[8,384]{1,0:T(8,128)(2,1)S(1)} fusion(bf16[384,384]{1,0:T(8,128)(2,1)} %param.26, bf16[8,384]{1,0:T(8,128)(2,1)} %param.21, f32[8]{0:T(128)S(1)} %add_rsqrt_fusion.3, f32[8]{0:T(128)S(1)} %broadcast_multiply_fusion.4), kind=kOutput, calls=%fused_computation.20 | convolution fusion | flops 2374656 | bytes 307264 | tf_op jit(solution)/shard_map/dot_general | solution.py:73
  37.2 0.7 broadcast_compare_fusion
  37.9 17.7 %all_gather.9 = bf16[128,384]{1,0:T(8,128)(2,1)S(1)} all-gather(bf16[8,384]{1,0:T(8,128)(2,1)S(1)} %convolution_convert_fusion.1), channel_id=1, replica_groups=mesh['groups'=2,'rows'=16] {'rows'}, dimensions={0}, use_global_device_ids=true | all-gather | bytes 104448 | tf_op jit(solution)/shard_map/all_gather | solution.py:89
  55.6 0.1 copy.28
  55.7 0.1 reshape.245
  55.8 0.0 copy-done.9
  55.9 0.1 dynamic_slice.9
  55.9 0.1 fusion.37
  56.0 0.0 copy-done.7
  56.0 0.0 copy-done.8
  56.0 0.1 add_select_fusion
  56.1 0.0 all-to-all-done
  56.1 0.0 copy-done.3
  56.1 0.4 fusion.49
  56.6 0.4 multiply_reduce_fusion.2
  56.9 0.0 copy-done.6
  57.0 0.5 fusion.13
  57.4 0.2 fusion.50
  57.7 0.2 fusion.20
  57.8 0.2 fusion.2
  58.1 0.1 reshape.248
  58.2 0.0 copy-done
  58.2 0.0 copy-done.2
  58.2 0.0 copy-done.11
  58.2 0.5 convert_reduce_fusion.1
  58.7 0.0 copy-start.5
  58.7 0.0 copy-start.1
  58.7 0.2 fusion.32
  58.9 0.0 copy-done.14
  58.9 0.2 convolution_convert_fusion.3
  59.1 18.8 %all_gather.11 = bf16[128,128]{1,0:T(8,128)(2,1)S(1)} all-gather(bf16[8,128]{1,0:T(8,128)(2,1)S(1)} %convolution_convert_fusion.3), channel_id=1, replica_groups=mesh['groups'=2,'rows'=16] {'rows'}, dimensions={0}, use_global_device_ids=true | all-gather | bytes 34816 | tf_op jit(solution)/shard_map/all_gather | solution.py:121
  77.9 0.0 copy-done.15
  77.9 0.2 fusion.11
  78.1 0.2 fusion.48
  78.3 1.0 %copy.34 = f32[1024,128]{0,1:T(8,128)} copy(f32[1024,128]{1,0:T(8,128)S(1)} %bitcast.47) | data formatting | bytes 1048576 | tf_op jit(solution)/shard_map/reshape | solution.py:28
  79.3 0.4 multiply_reduce_fusion.1
  79.7 0.3 multiply_convert_fusion.2
  80.1 0.0 copy-done.1
  80.1 0.4 fusion.55
  80.5 0.0 copy-done.5
  80.5 0.0 copy-start.4
  80.6 0.0 copy-start.10
  80.6 2.0 %fusion.53 = (f32[1024]{0:T(1024)S(1)}, f32[1024,128]{0,1:T(8,128)S(1)}) fusion(f32[1024,128]{0,1:T(8,128)} %copy.34, bf16[512,128]{1,0:T(8,128)(2,1)S(1)} %copy-done.12, f32[1024,512]{1,0:T(8,128)S(1)} %fusion.55, bf16[1024,128]{1,0:T(8,128)(2,1)S(1)} %multiply_convert_fusion.2, bf16[128,512]{1,0:T(8,128)(2,1)S(1)} %copy-done.13), kind=kOutput, calls=%fused_computation.87 | convolution fusion | flops 271842304 | bytes 3674112 | tf_op jit(solution)/shard_map/dot_general | solution.py:33
  82.5 0.1 multiply_reduce_fusion
  82.6 0.0 copy-done.4
  82.6 0.0 copy-done.10
  82.6 0.2 fusion.54
  82.9 0.1 fusion.18
  82.9 0.7 multiply_reduce_fusion.3
  (23 shorter events, 0.1 us)
Async XLA Ops:
  0.6 57.6 %copy-start = (bf16[384,384]{1,0:T(8,128)(2,1)S(1)}, bf16[384,384]{1,0:T(8,128)(2,1)}, u32[]{:S(2)}) copy-start(bf16[384,384]{1,0:T(8,128)(2,1)} %param.30) | copy-start | bytes 884740
  0.6 55.4 %copy-start.7 = (s32[128]{0:T(128)S(1)}, s32[128]{0:T(128)}, u32[]{:S(2)}) copy-start(s32[128]{0:T(128)} %param.22) | copy-start | bytes 1540
  0.7 55.4 %copy-start.8 = (s32[128]{0:T(128)S(1)}, s32[128]{0:T(128)}, u32[]{:S(2)}) copy-start(s32[128]{0:T(128)} %param.23) | copy-start | bytes 1540
  0.7 55.2 %copy-start.9 = (s32[128]{0:T(128)S(1)}, s32[128]{0:T(128)}, u32[]{:S(2)}) copy-start(s32[128]{0:T(128)} %param.24) | copy-start | bytes 1540
  0.7 55.4 %copy-start.3 = (bf16[66,128]{1,0:T(8,128)(2,1)S(1)}, bf16[66,128]{1,0:T(8,128)(2,1)}, u32[]{:S(2)}) copy-start(bf16[66,128]{1,0:T(8,128)(2,1)} %param.32) | copy-start | bytes 50692
  0.7 56.3 %copy-start.6 = (bf16[128,16]{0,1:T(8,128)(2,1)S(1)}, bf16[128,16]{0,1:T(8,128)(2,1)}, u32[]{:S(2)}) copy-start(bf16[128,16]{0,1:T(8,128)(2,1)} %param.31) | copy-start | bytes 12292
  0.7 55.4 %all-to-all-start = ((bf16[128,8,128]{2,1,0:T(8,128)(2,1)}), bf16[128,8,128]{2,1,0:T(8,128)(2,1)S(1)}, u32[]{:S(2)}, u32[]{:S(2)}) async-start(bf16[128,8,128]{2,1,0:T(8,128)(2,1)} %param.20), calls=%async_computation | async-start | bytes 524288 | tf_op jit(solution)/shard_map/all_to_all | solution.py:77
  11.1 47.1 %copy-start.2 = (bf16[8,384]{1,0:T(8,128)(2,1)S(1)}, bf16[8,384]{1,0:T(8,128)(2,1)}, u32[]{:S(2)}) copy-start(bf16[8,384]{1,0:T(8,128)(2,1)} %param.21) | copy-start | bytes 18436
  11.1 47.1 %copy-start.11 = (bf16[384,384]{1,0:T(8,128)(2,1)S(1)}, bf16[384,384]{1,0:T(8,128)(2,1)}, u32[]{:S(2)}) copy-start(bf16[384,384]{1,0:T(8,128)(2,1)} %param.29) | copy-start | bytes 884740
  36.0 22.9 %copy-start.14 = (bf16[384,128]{1,0:T(8,128)(2,1)S(1)}, bf16[384,128]{1,0:T(8,128)(2,1)}, u32[]{:S(2)}) copy-start(bf16[384,128]{1,0:T(8,128)(2,1)} %param.34) | copy-start | bytes 294916
  37.2 40.7 %copy-start.15 = (bf16[384,128]{1,0:T(8,128)(2,1)S(1)}, bf16[384,128]{1,0:T(8,128)(2,1)}, u32[]{:S(2)}) copy-start(bf16[384,128]{1,0:T(8,128)(2,1)} %param.33) | copy-start | bytes 294916
  58.7 21.8 %copy-start.5 = (bf16[8,384]{1,0:T(8,128)(2,1)}, bf16[8,384]{1,0:T(8,128)(2,1)S(1)}, u32[]{:S(2)}) copy-start(bf16[8,384]{1,0:T(8,128)(2,1)S(1)} %get-tuple-element.11) | copy-start | bytes 18436
  58.7 21.4 %copy-start.1 = (bf16[128,512]{1,0:T(8,128)(2,1)S(1)}, bf16[128,512]{1,0:T(8,128)(2,1)}, u32[]{:S(2)}) copy-start(bf16[128,512]{1,0:T(8,128)(2,1)} %param.36) | copy-start | bytes 393220
  79.3 1.2 %copy-start.12 = (bf16[512,128]{1,0:T(8,128)(2,1)S(1)}, bf16[512,128]{1,0:T(8,128)(2,1)}, u32[]{:S(2)}) copy-start(bf16[512,128]{1,0:T(8,128)(2,1)} %param.37) | copy-start | bytes 393220
  79.3 1.2 %copy-start.13 = (bf16[128,512]{1,0:T(8,128)(2,1)S(1)}, bf16[128,512]{1,0:T(8,128)(2,1)}, u32[]{:S(2)}) copy-start(bf16[128,512]{1,0:T(8,128)(2,1)} %param.35) | copy-start | bytes 393220
  80.5 2.1 %copy-start.4 = (bf16[128,64]{0,1:T(8,128)(2,1)S(1)}, bf16[128,64]{0,1:T(8,128)(2,1)}, u32[]{:S(2)}) copy-start(bf16[128,64]{0,1:T(8,128)(2,1)} %param.38) | copy-start | bytes 49156
  80.6 2.1 %copy-start.10 = (f32[64]{0:T(128)S(1)}, f32[64]{0:T(128)}, u32[]{:S(2)}) copy-start(f32[64]{0:T(128)} %param.39) | copy-start | bytes 772
where the time goes:
time: 84.1 us; the launch traced here: 83.6 us
  blocking collectives  58.6 us (70%)
  matrix products  8.32 us (10%)
  starting transfers between devices  7.53 us (9%)
  other arithmetic  5.09 us (6%)
  local copies, waits for them, and re-layouts  3.06 us (4%)
  between operations  0.98 us (1%)
    all_gather x1, blocking collectives, on_device(): value_part = lax.all_gather(values_local, 'rows', axis=0, tiled=True)  22.1 us
    all_gather x1, blocking collectives, on_device(): every_b = lax.all_gather(factor_b, 'rows', axis=0, tiled=True)  18.8 us
    all_gather x1, blocking collectives, on_device(): key_part = lax.all_gather(keys_local, 'rows', axis=0, tiled=True)  17.7 us
    all_to_all x1, starting transfers between devices, on_device(): lax.all_to_all(pair_repr, 'rows', split_axis=0, concat_axis=1, tiled=True)  7.53 us
    dot_general x1, matrix products, pair_tail(): jnp.dot(hidden, w_hidden_out, preferred_element_type=jnp.float32)  1.96 us
    reduce_sum x5, other arithmetic, norm_rows(): spread = jnp.mean(center * center, axis=-1, keepdims=True)  1.87 us
  transfers between devices with their start and end apart: 1, of which 0 were waited for; matrix products, arithmetic and copies ran while one was open for 10% of the time, Pallas kernels for 0%

commit v1 on v0

--- a/solution.py
+++ b/solution.py
@@ -1,3 +1,4 @@
+import functools
 import math
 import jax
 import jax.numpy as jnp
@@ -6,6 +7,21 @@
 
 epsilon = 1e-05
 masked_score = -1e30
+
+
+def state_see(load, array_dim, out_dim):
+    return jnp.concatenate(
+        jax.lax.all_to_all(
+            jnp.stack(jnp.split(load, jax.lax.axis_size("rows"), axis=array_dim), axis=0),
+            axis_name="rows",
+            split_axis=0,
+            concat_axis=0,
+        ),
+        axis=out_dim,
+    )
+
+
+fit_points = functools.partial(state_see, array_dim=0, out_dim=1)
 
 
 def norm_rows(values):
@@ -74,7 +90,7 @@
     keys_local = jnp.dot(normed, w_key, preferred_element_type=jnp.float32).astype(jnp.bfloat16)
     values_local = jnp.dot(normed, w_value, preferred_element_type=jnp.float32).astype(jnp.bfloat16)
     gating = jax.nn.sigmoid(jnp.dot(normed, w_gate, preferred_element_type=jnp.float32))
-    pair_local = lax.all_to_all(pair_repr, "rows", split_axis=0, concat_axis=1, tiled=True)
+    pair_local = fit_points(pair_repr)
     pair_in = pair_local.astype(jnp.float32) + relative(
         res_local, chain_local, residue_index, chain_index, rel_table
     )

time: 84.1 us -> 106 us (1.26); the launches traced: 83.6 us -> 104 us
  local copies, waits for them, and re-layouts: 3.06 us -> 24.2 us
    unnamed x32 -> x49, local copies, waits for them, and re-layouts: 0.08 us -> 19.9 us
    another operation x0 -> x1, local copies, waits for them, and re-layouts: none -> 1.32 us  [state_see(): jnp.stack(jnp.split(load, jax.lax.axis_size('rows'), axis=array_dim), axi...]
  transfers between devices with their start and end apart: 1 -> 1, of which waited for: 0 -> 0; matrix products, arithmetic and copies ran while one was open for 10% -> 7% of each run, Pallas kernels for 0% -> 0%
where the time goes in v1:
time: 106 us; the launch traced here: 104 us
  blocking collectives  58.8 us (55%)
  local copies, waits for them, and re-layouts  24.2 us (23%)
  matrix products  8.32 us (8%)
  starting transfers between devices  7.39 us (7%)
  other arithmetic  4.39 us (4%)
    all_gather x1, blocking collectives, on_device(): value_part = lax.all_gather(values_local, 'rows', axis=0, tiled=True)  22.1 us
    unnamed x49, local copies, waits for them, and re-layouts  19.9 us
    all_gather x1, blocking collectives, on_device(): every_b = lax.all_gather(factor_b, 'rows', axis=0, tiled=True)  18.8 us
    all_gather x1, blocking collectives, on_device(): key_part = lax.all_gather(keys_local, 'rows', axis=0, tiled=True)  17.8 us
    all_to_all x1, starting transfers between devices, state_see(): jax.lax.all_to_all(jnp.stack(jnp.split(load, jax.lax.axis_size('rows'), a...  7.39 us
  transfers between devices with their start and end apart: 1, of which 0 were waited for; matrix products, arithmetic and copies ran while one was open for 7% of the time, Pallas kernels for 0%

profile of v1, /device:TPU:0, one launch (start us, length us, event | category | flops | bytes accessed | tf_op | source)
XLA Modules:
  0.0 104.1 jit_solution(6689962023301109946)
XLA Ops:
  0.6 0.0 copy-start
  0.6 0.0 copy-start.7
  0.7 0.0 copy-start.8
  0.7 0.0 copy-start.16
  0.7 0.0 copy-start.9
  0.7 1.4 %constant_dynamic-update-slice_fusion.15 = bf16[16,8,8,128]{3,2,1,0:T(8,128)(2,1)} fusion(bf16[128,8,128]{2,1,0:T(8,128)(2,1)} %param.20), kind=kLoop, calls=%fused_computation.62 | loop fusion | bytes 32768
  2.1 1.3 %constant_dynamic-update-slice_fusion.14 = bf16[16,8,8,128]{3,2,1,0:T(8,128)(2,1)} fusion(bf16[16,8,8,128]{3,2,1,0:T(8,128)(2,1)} %constant_dynamic-update-slice_fusion.15, bf16[128,8,128]{2,1,0:T(8,128)(2,1)} %param.20), kind=kLoop, calls=%fused_computation.61 | loop fusion | bytes 32768
  3.4 1.3 %constant_dynamic-update-slice_fusion.13 = bf16[16,8,8,128]{3,2,1,0:T(8,128)(2,1)} fusion(bf16[16,8,8,128]{3,2,1,0:T(8,128)(2,1)} %constant_dynamic-update-slice_fusion.14, bf16[128,8,128]{2,1,0:T(8,128)(2,1)} %param.20), kind=kLoop, calls=%fused_computation.60 | loop fusion | bytes 32768
  4.7 1.3 %constant_dynamic-update-slice_fusion.12 = bf16[16,8,8,128]{3,2,1,0:T(8,128)(2,1)} fusion(bf16[16,8,8,128]{3,2,1,0:T(8,128)(2,1)} %constant_dynamic-update-slice_fusion.13, bf16[128,8,128]{2,1,0:T(8,128)(2,1)} %param.20), kind=kLoop, calls=%fused_computation.59 | loop fusion | bytes 32768
  6.1 1.3 %constant_dynamic-update-slice_fusion.11 = bf16[16,8,8,128]{3,2,1,0:T(8,128)(2,1)} fusion(bf16[16,8,8,128]{3,2,1,0:T(8,128)(2,1)} %constant_dynamic-update-slice_fusion.12, bf16[128,8,128]{2,1,0:T(8,128)(2,1)} %param.20), kind=kLoop, calls=%fused_computation.58 | loop fusion | bytes 32768
  7.4 1.3 %constant_dynamic-update-slice_fusion.10 = bf16[16,8,8,128]{3,2,1,0:T(8,128)(2,1)} fusion(bf16[16,8,8,128]{3,2,1,0:T(8,128)(2,1)} %constant_dynamic-update-slice_fusion.11, bf16[128,8,128]{2,1,0:T(8,128)(2,1)} %param.20), kind=kLoop, calls=%fused_computation.57 | loop fusion | bytes 32768
  8.7 1.3 %constant_dynamic-update-slice_fusion.9 = bf16[16,8,8,128]{3,2,1,0:T(8,128)(2,1)} fusion(bf16[16,8,8,128]{3,2,1,0:T(8,128)(2,1)} %constant_dynamic-update-slice_fusion.10, bf16[128,8,128]{2,1,0:T(8,128)(2,1)} %param.20), kind=kLoop, calls=%fused_computation.56 | loop fusion | bytes 32768
  10.0 1.3 %constant_dynamic-update-slice_fusion.8 = bf16[16,8,8,128]{3,2,1,0:T(8,128)(2,1)} fusion(bf16[16,8,8,128]{3,2,1,0:T(8,128)(2,1)} %constant_dynamic-update-slice_fusion.9, bf16[128,8,128]{2,1,0:T(8,128)(2,1)} %param.20), kind=kLoop, calls=%fused_computation.55 | loop fusion | bytes 32768
  11.3 1.3 %constant_dynamic-update-slice_fusion.7 = bf16[16,8,8,128]{3,2,1,0:T(8,128)(2,1)} fusion(bf16[16,8,8,128]{3,2,1,0:T(8,128)(2,1)} %constant_dynamic-update-slice_fusion.8, bf16[128,8,128]{2,1,0:T(8,128)(2,1)} %param.20), kind=kLoop, calls=%fused_computation.54 | loop fusion | bytes 32768
  12.6 1.3 %constant_dynamic-update-slice_fusion.6 = bf16[16,8,8,128]{3,2,1,0:T(8,128)(2,1)} fusion(bf16[16,8,8,128]{3,2,1,0:T(8,128)(2,1)} %constant_dynamic-update-slice_fusion.7, bf16[128,8,128]{2,1,0:T(8,128)(2,1)} %param.20), kind=kLoop, calls=%fused_computation.53 | loop fusion | bytes 32768
  13.9 1.3 %constant_dynamic-update-slice_fusion.5 = bf16[16,8,8,128]{3,2,1,0:T(8,128)(2,1)} fusion(bf16[16,8,8,128]{3,2,1,0:T(8,128)(2,1)} %constant_dynamic-update-slice_fusion.6, bf16[128,8,128]{2,1,0:T(8,128)(2,1)} %param.20), kind=kLoop, calls=%fused_computation.52 | loop fusion | bytes 32768
  15.3 1.3 %constant_dynamic-update-slice_fusion.4 = bf16[16,8,8,128]{3,2,1,0:T(8,128)(2,1)} fusion(bf16[16,8,8,128]{3,2,1,0:T(8,128)(2,1)} %constant_dynamic-update-slice_fusion.5, bf16[128,8,128]{2,1,0:T(8,128)(2,1)} %param.20), kind=kLoop, calls=%fused_computation.51 | loop fusion | bytes 32768
  16.6 1.3 %constant_dynamic-update-slice_fusion.3 = bf16[16,8,8,128]{3,2,1,0:T(8,128)(2,1)} fusion(bf16[16,8,8,128]{3,2,1,0:T(8,128)(2,1)} %constant_dynamic-update-slice_fusion.4, bf16[128,8,128]{2,1,0:T(8,128)(2,1)} %param.20), kind=kLoop, calls=%fused_computation.50 | loop fusion | bytes 32768
  17.9 1.3 %constant_dynamic-update-slice_fusion.2 = bf16[16,8,8,128]{3,2,1,0:T(8,128)(2,1)} fusion(bf16[16,8,8,128]{3,2,1,0:T(8,128)(2,1)} %constant_dynamic-update-slice_fusion.3, bf16[128,8,128]{2,1,0:T(8,128)(2,1)} %param.20), kind=kLoop, calls=%fused_computation.49 | loop fusion | bytes 32768
  19.2 1.3 %constant_dynamic-update-slice_fusion.1 = bf16[16,8,8,128]{3,2,1,0:T(8,128)(2,1)} fusion(bf16[16,8,8,128]{3,2,1,0:T(8,128)(2,1)} %constant_dynamic-update-slice_fusion.2, bf16[128,8,128]{2,1,0:T(8,128)(2,1)} %param.20), kind=kLoop, calls=%fused_computation.48 | loop fusion | bytes 32768
  20.5 1.3 %constant_dynamic-update-slice_fusion = bf16[16,8,8,128]{3,2,1,0:T(8,128)(2,1)} fusion(bf16[16,8,8,128]{3,2,1,0:T(8,128)(2,1)} %constant_dynamic-update-slice_fusion.1, bf16[128,8,128]{2,1,0:T(8,128)(2,1)} %param.20), kind=kLoop, calls=%fused_computation.47 | loop fusion | bytes 32768 | tf_op jit(solution)/shard_map/stack | solution.py:15
  21.9 7.4 %all-to-all-start = ((bf16[16,8,8,128]{3,2,1,0:T(8,128)(2,1)}), bf16[16,8,8,128]{3,2,1,0:T(8,128)(2,1)S(1)}, u32[]{:S(2)}, u32[]{:S(2)}) async-start(bf16[16,8,8,128]{3,2,1,0:T(8,128)(2,1)} %constant_dynamic-update-slice_fusion), calls=%async_computation | async-start | bytes 524288 | tf_op jit(solution)/shard_map/all_to_all | solution.py:14
  29.3 0.8 convert_reduce_fusion
  30.1 0.9 fusion.30
  31.0 1.2 %convolution_convert_fusion = bf16[8,384]{1,0:T(8,128)(2,1)S(1)} fusion(bf16[384,384]{1,0:T(8,128)(2,1)} %param.28, bf16[8,384]{1,0:T(8,128)(2,1)} %param.21, f32[8]{0:T(128)S(1)} %add_rsqrt_fusion.3, f32[8]{0:T(128)S(1)} %broadcast_multiply_fusion.4), kind=kOutput, calls=%fused_computation.18 | convolution fusion | flops 2374656 | bytes 307264 | tf_op jit(solution)/shard_map/dot_general | solution.py:91
  32.2 22.1 %all_gather.10 = bf16[128,384]{1,0:T(8,128)(2,1)S(1)} all-gather(bf16[8,384]{1,0:T(8,128)(2,1)S(1)} %convolution_convert_fusion), channel_id=1, replica_groups=mesh['groups'=2,'rows'=16] {'rows'}, dimensions={0}, use_global_device_ids=true | all-gather | bytes 104448 | tf_op jit(solution)/shard_map/all_gather | solution.py:106
  54.3 0.1 copy.32
  54.4 0.7 dynamic_slice.11
  55.1 0.7 dynamic_slice.10
  55.9 1.2 %convolution_convert_fusion.1 = bf16[8,384]{1,0:T(8,128)(2,1)S(1)} fusion(bf16[384,384]{1,0:T(8,128)(2,1)} %param.27, bf16[8,384]{1,0:T(8,128)(2,1)} %param.21, f32[8]{0:T(128)S(1)} %add_rsqrt_fusion.3, f32[8]{0:T(128)S(1)} %broadcast_multiply_fusion.4), kind=kOutput, calls=%fused_computation.19 | convolution fusion | flops 2374656 | bytes 307264 | tf_op jit(solution)/shard_map/dot_general | solution.py:90
  57.0 1.2 %convolution_convert_fusion.2 = bf16[8,384]{1,0:T(8,128)(2,1)S(1)} fusion(bf16[384,384]{1,0:T(8,128)(2,1)} %param.26, bf16[8,384]{1,0:T(8,128)(2,1)} %param.21, f32[8]{0:T(128)S(1)} %add_rsqrt_fusion.3, f32[8]{0:T(128)S(1)} %broadcast_multiply_fusion.4), kind=kOutput, calls=%fused_computation.20 | convolution fusion | flops 2374656 | bytes 307264 | tf_op jit(solution)/shard_map/dot_general | solution.py:89
  58.3 17.8 %all_gather.9 = bf16[128,384]{1,0:T(8,128)(2,1)S(1)} all-gather(bf16[8,384]{1,0:T(8,128)(2,1)S(1)} %convolution_convert_fusion.1), channel_id=1, replica_groups=mesh['groups'=2,'rows'=16] {'rows'}, dimensions={0}, use_global_device_ids=true | all-gather | bytes 104448 | tf_op jit(solution)/shard_map/all_gather | solution.py:105
  76.1 0.1 copy.28
  76.2 0.1 reshape.245
  76.3 0.1 dynamic_slice.9
  76.4 0.1 fusion.37
  76.5 0.1 add_select_fusion
  76.6 0.0 all-to-all-done
  76.6 0.4 fusion.49
  77.0 0.4 multiply_reduce_fusion.2
  77.4 0.5 fusion.13
  77.9 0.2 fusion.50
  78.1 0.2 fusion.20
  78.3 0.2 fusion.2
  78.6 0.1 reshape.248
  78.7 0.5 convert_reduce_fusion.1
  79.2 0.0 copy-start.5
  79.2 0.0 copy-start.1
  79.2 0.2 fusion.32
  79.4 0.2 convolution_convert_fusion.3
  79.6 18.8 %all_gather.11 = bf16[128,128]{1,0:T(8,128)(2,1)S(1)} all-gather(bf16[8,128]{1,0:T(8,128)(2,1)S(1)} %convolution_convert_fusion.3), channel_id=1, replica_groups=mesh['groups'=2,'rows'=16] {'rows'}, dimensions={0}, use_global_device_ids=true | all-gather | bytes 34816 | tf_op jit(solution)/shard_map/all_gather | solution.py:137
  98.4 0.2 fusion.11
  98.6 0.2 fusion.48
  98.8 1.0 copy.34
  99.8 0.4 multiply_reduce_fusion.1
  100.2 0.3 multiply_convert_fusion.2
  100.6 0.4 fusion.55
  101.0 0.0 copy-start.4
  101.0 0.0 copy-start.10
  101.1 2.0 %fusion.53 = (f32[1024]{0:T(1024)S(1)}, f32[1024,128]{0,1:T(8,128)S(1)}) fusion(f32[1024,128]{0,1:T(8,128)} %copy.34, bf16[512,128]{1,0:T(8,128)(2,1)S(1)} %copy-done.12, f32[1024,512]{1,0:T(8,128)S(1)} %fusion.55, bf16[1024,128]{1,0:T(8,128)(2,1)S(1)} %multiply_convert_fusion.2, bf16[128,512]{1,0:T(8,128)(2,1)S(1)} %copy-done.13), kind=kOutput, calls=%fused_computation.104 | convolution fusion | flops 271842304 | bytes 3674112 | tf_op jit(solution)/shard_map/dot_general | solution.py:49
  103.0 0.1 multiply_reduce_fusion
  103.1 0.2 fusion.54
  103.3 0.1 fusion.18
  103.4 0.7 multiply_reduce_fusion.3
  (41 shorter events, 0.2 us)
Async XLA Ops:
  0.6 78.0 %copy-start = (bf16[384,384]{1,0:T(8,128)(2,1)S(1)}, bf16[384,384]{1,0:T(8,128)(2,1)}, u32[]{:S(2)}) copy-start(bf16[384,384]{1,0:T(8,128)(2,1)} %param.30) | copy-start | bytes 884740
  0.6 75.9 %copy-start.7 = (s32[128]{0:T(128)S(1)}, s32[128]{0:T(128)}, u32[]{:S(2)}) copy-start(s32[128]{0:T(128)} %param.22) | copy-start | bytes 1540
  0.7 75.8 %copy-start.8 = (s32[128]{0:T(128)S(1)}, s32[128]{0:T(128)}, u32[]{:S(2)}) copy-start(s32[128]{0:T(128)} %param.23) | copy-start | bytes 1540
  0.7 57.6 %copy-start.16 = (s32[128]{0:T(128)S(1)}, s32[128]{0:T(128)}, u32[]{:S(2)}) copy-start(s32[128]{0:T(128)} %param.25) | copy-start | bytes 1540
  0.7 75.7 %copy-start.9 = (s32[128]{0:T(128)S(1)}, s32[128]{0:T(128)}, u32[]{:S(2)}) copy-start(s32[128]{0:T(128)} %param.24) | copy-start | bytes 1540
  0.7 75.9 %copy-start.3 = (bf16[66,128]{1,0:T(8,128)(2,1)S(1)}, bf16[66,128]{1,0:T(8,128)(2,1)}, u32[]{:S(2)}) copy-start(bf16[66,128]{1,0:T(8,128)(2,1)} %param.32) | copy-start | bytes 50692
  0.7 76.7 %copy-start.6 = (bf16[128,16]{0,1:T(8,128)(2,1)S(1)}, bf16[128,16]{0,1:T(8,128)(2,1)}, u32[]{:S(2)}) copy-start(bf16[128,16]{0,1:T(8,128)(2,1)} %param.31) | copy-start | bytes 12292
  21.9 54.7 %all-to-all-start = ((bf16[16,8,8,128]{3,2,1,0:T(8,128)(2,1)}), bf16[16,8,8,128]{3,2,1,0:T(8,128)(2,1)S(1)}, u32[]{:S(2)}, u32[]{:S(2)}) async-start(bf16[16,8,8,128]{3,2,1,0:T(8,128)(2,1)} %constant_dynamic-update-slice_fusion), calls=%async_computation | async-start | bytes 524288 | tf_op jit(solution)/shard_map/all_to_all | solution.py:14
  32.1 46.5 %copy-start.2 = (bf16[8,384]{1,0:T(8,128)(2,1)S(1)}, bf16[8,384]{1,0:T(8,128)(2,1)}, u32[]{:S(2)}) copy-start(bf16[8,384]{1,0:T(8,128)(2,1)} %param.21) | copy-start | bytes 18436
  32.1 46.5 %copy-start.11 = (bf16[384,384]{1,0:T(8,128)(2,1)S(1)}, bf16[384,384]{1,0:T(8,128)(2,1)}, u32[]{:S(2)}) copy-start(bf16[384,384]{1,0:T(8,128)(2,1)} %param.29) | copy-start | bytes 884740
  57.0 22.4 %copy-start.14 = (bf16[384,128]{1,0:T(8,128)(2,1)S(1)}, bf16[384,128]{1,0:T(8,128)(2,1)}, u32[]{:S(2)}) copy-start(bf16[384,128]{1,0:T(8,128)(2,1)} %param.34) | copy-start | bytes 294916
  58.2 40.2 %copy-start.15 = (bf16[384,128]{1,0:T(8,128)(2,1)S(1)}, bf16[384,128]{1,0:T(8,128)(2,1)}, u32[]{:S(2)}) copy-start(bf16[384,128]{1,0:T(8,128)(2,1)} %param.33) | copy-start | bytes 294916
  79.2 21.8 %copy-start.5 = (bf16[8,384]{1,0:T(8,128)(2,1)}, bf16[8,384]{1,0:T(8,128)(2,1)S(1)}, u32[]{:S(2)}) copy-start(bf16[8,384]{1,0:T(8,128)(2,1)S(1)} %get-tuple-element.11) | copy-start | bytes 18436
  79.2 21.4 %copy-start.1 = (bf16[128,512]{1,0:T(8,128)(2,1)S(1)}, bf16[128,512]{1,0:T(8,128)(2,1)}, u32[]{:S(2)}) copy-start(bf16[128,512]{1,0:T(8,128)(2,1)} %param.36) | copy-start | bytes 393220
  99.8 1.2 %copy-start.12 = (bf16[512,128]{1,0:T(8,128)(2,1)S(1)}, bf16[512,128]{1,0:T(8,128)(2,1)}, u32[]{:S(2)}) copy-start(bf16[512,128]{1,0:T(8,128)(2,1)} %param.37) | copy-start | bytes 393220
  99.8 1.2 %copy-start.13 = (bf16[128,512]{1,0:T(8,128)(2,1)S(1)}, bf16[128,512]{1,0:T(8,128)(2,1)}, u32[]{:S(2)}) copy-start(bf16[128,512]{1,0:T(8,128)(2,1)} %param.35) | copy-start | bytes 393220
  101.0 2.1 %copy-start.4 = (bf16[128,64]{0,1:T(8,128)(2,1)S(1)}, bf16[128,64]{0,1:T(8,128)(2,1)}, u32[]{:S(2)}) copy-start(bf16[128,64]{0,1:T(8,128)(2,1)} %param.38) | copy-start | bytes 49156
  101.0 2.1 %copy-start.10 = (f32[64]{0:T(128)S(1)}, f32[64]{0:T(128)}, u32[]{:S(2)}) copy-start(f32[64]{0:T(128)} %param.39) | copy-start | bytes 772
